TPU v7x, 128 devices: a whole 4x4x4 slice. The times are simulated.
128 devices in a mesh: coarse: 2 (over z_hi), fine: 8 (over z_lo, y), model: 8 (over x, core).
Axes of the slice: x: 4, y: 4, z: 4 (z_hi: 2, z_lo: 2; z = z_hi * 2 + z_lo), core: 2. Of those that a mesh axis runs over, the one named last changes fastest.
Arguments:
- fresh_keys: bfloat16 [16, 24576, 8, 128], P(None, ('coarse', 'fine'), 'model'), may hold values from -6 to 6
- fresh_values: bfloat16 [16, 24576, 8, 128], P(None, ('coarse', 'fine'), 'model'), may hold values from -6 to 6
- turn_angle: float32 [24576, 64], replicated, may hold values from -3.140625 to 3.140625
Outputs:
- cache_keys: bfloat16 [16, 24576, 8, 128], P(('coarse', 'fine'), None, 'model')
- cache_values: bfloat16 [16, 24576, 8, 128], P(('coarse', 'fine'), None, 'model')
- page_high: bfloat16 [16, 768, 8, 128], P(('coarse', 'fine'), None, 'model')
- page_low: bfloat16 [16, 768, 8, 128], P(('coarse', 'fine'), None, 'model')
All inputs are finite; a program needn't handle non-finite values.
Results may differ from a plain program's by a relative error of at most 0.001.
Values may be sent and summed in bfloat16 or wider, within the bound.
A program may use at most 128 MiB of HBM per device.

v0:
```python
import jax
import jax.numpy as jnp
from jax import lax
from jax.sharding import PartitionSpec as P

PAGE = 32


def in_one_piece(arrays, axis, split_dim, concat_dim, along):
    ends, at = ([], 0)
    for a in arrays[:-1]:
        at += a.shape[along]
        ends.append(at)
    both = jnp.concatenate(arrays, axis=along)
    return tuple(
        jnp.split(
            lax.all_to_all(both, axis, split_axis=split_dim, concat_axis=concat_dim, tiled=True),
            ends,
            axis=along,
        )
    )


def turn_pairs(vectors, angle):
    half = vectors.shape[-1] // 2
    cosine, sine = (jnp.cos(angle)[None, :, None, :], jnp.sin(angle)[None, :, None, :])
    first, second = (vectors[..., :half], vectors[..., half:])
    return jnp.concatenate(
        [first * cosine - second * sine, second * cosine + first * sine], axis=-1
    )


def prepare_keys(plain_keys, angle):
    wide_keys = plain_keys.astype(jnp.float32)
    return turn_pairs(wide_keys, angle)


def on_device(fresh_keys, fresh_values, turn_angle):
    my_angles = lax.dynamic_slice_in_dim(
        turn_angle, lax.axis_index(("coarse", "fine")) * fresh_keys.shape[1], fresh_keys.shape[1]
    )
    sent_keys = prepare_keys(fresh_keys, my_angles).astype(jnp.bfloat16)
    moved_keys, cache_values = in_one_piece((sent_keys, fresh_values), ("coarse", "fine"), 0, 1, 2)
    page_view = moved_keys.reshape(
        moved_keys.shape[0], -1, PAGE, moved_keys.shape[2], moved_keys.shape[3]
    )
    page_high = jnp.max(page_view, axis=2)
    page_low = jnp.min(page_view, axis=2)
    return (moved_keys, cache_values, page_high, page_low)


def solution(mesh):
    return jax.shard_map(
        on_device,
        mesh=mesh,
        in_specs=(
            P(None, ("coarse", "fine"), "model", None),
            P(None, ("coarse", "fine"), "model", None),
            P(),
        ),
        out_specs=(
            P(("coarse", "fine"), None, "model", None),
            P(("coarse", "fine"), None, "model", None),
            P(("coarse", "fine"), None, "model", None),
            P(("coarse", "fine"), None, "model", None),
        ),
        check_vma=False,
    )
```

profile of v0, /device:TPU:0, one launch (start us, length us, event | category | flops | bytes accessed | tf_op | source)
XLA Modules:
  0.0 182.6 jit_solution(2764367730118668713)
XLA Ops:
  0.6 2.3 %dynamic-slice_cosine_fusion = (f32[1536,64]{0,1:T(8,128)S(1)}, f32[1536,64]{0,1:T(8,128)S(1)}) fusion(f32[24576,64]{0,1:T(8,128)} %param.5, s32[]{:T(128)S(6)} %select_n.3), kind=kLoop, calls=%fused_computation.4 | loop fusion | bytes 1179652 | tf_op jit(solution)/shard_map/cos | solution.py:26
  3.0 1.2 copy.7
  4.1 1.2 copy.8
  5.3 4.0 %convert_element_type.12 = f32[16,1536,1,128]{3,1,2,0:T(8,128)S(1)} convert(bf16[16,1536,1,128]{3,1,2,0:T(8,128)(2,1)} %param.3) | non-fusion elementwise | flops 3145728 | bytes 18874368 | tf_op jit(solution)/shard_map/convert_element_type | solution.py:34
  9.3 5.5 %subtract_convert_fusion = (bf16[16,1536,1,64]{3,1,2,0:T(8,128)(2,1)S(1)}, bf16[16,1536,1,64]{3,1,2,0:T(8,128)(2,1)S(1)}) fusion(f32[16,1536,1,128]{3,1,2,0:T(8,128)S(1)} %convert_element_type.12, f32[1536,64]{1,0:T(8,128)} %copy.8, f32[1536,64]{1,0:T(8,128)} %copy.7), kind=kLoop, calls=%fused_computation.2 | loop fusion | flops 12582912 | bytes 19660800 | tf_op jit(solution)/shard_map/convert
  14.9 6.4 %pad_maximum_fusion = bf16[16,1536,2,128]{3,1,2,0:T(8,128)(2,1)S(1)} fusion(bf16[16,1536,1,128]{3,1,2,0:T(8,128)(2,1)} %param.4, bf16[16,1536,1,64]{3,1,2,0:T(8,128)(2,1)S(1)} %get-tuple-element.7, bf16[16,1536,1,64]{3,1,2,0:T(8,128)(2,1)S(1)} %get-tuple-element.6), kind=kLoop, calls=%fused_computation | loop fusion | flops 37748736 | bytes 25165824 | tf_op jit(solution)/shard_map/concatenate | solution.py:14
  21.3 148.7 %all_to_all.12 = bf16[16,1536,2,128]{3,1,2,0:T(8,128)(2,1)S(1)} all-to-all(bf16[16,1536,2,128]{3,1,2,0:T(8,128)(2,1)S(1)} %pad_maximum_fusion), channel_id=1, replica_groups=mesh['coarse'=2,'fine'=8,'model'=8] {'coarse','fine'}, dimensions={0} | all-to-all | bytes 25165824 | tf_op jit(solution)/shard_map/all_to_all | solution.py:17
  170.0 1.9 %copy.9 = bf16[16,1536,2,128]{3,1,0,2:T(8,128)(2,1)S(1)} copy(bf16[16,1536,2,128]{3,1,2,0:T(8,128)(2,1)S(1)} %all_to_all.12) | data formatting | bytes 25165824 | tf_op jit(solution)/shard_map/all_to_all | solution.py:17
  171.9 3.2 %fusion.1 = (bf16[1,24576,1,128]{3,1,2,0:T(8,128)(2,1)}, bf16[1,24576,1,128]{3,1,2,0:T(8,128)(2,1)S(1)}) fusion(bf16[1,24576,2,128]{3,1,2,0:T(8,128)(2,1)S(1)} %bitcast.4), kind=kLoop, calls=%fused_computation.6 | loop fusion | bytes 25165824 | tf_op jit(solution)/shard_map/split | solution.py:16
  175.2 0.0 copy-start
  175.2 7.5 %fusion = (bf16[768,128]{1,0:T(8,128)(2,1)}, bf16[768,128]{1,0:T(8,128)(2,1)}) fusion(bf16[1,768,32,1,128]{4,2,1,3,0:T(8,128)(2,1)S(1)} %bitcast.5), kind=kLoop, calls=%fused_computation.5 | loop fusion | flops 6094848 | bytes 6684672 | tf_op jit(solution)/shard_map/reduce_min | solution.py:48
  182.6 0.0 copy-done
Async XLA Ops:
  175.2 7.5 %copy-start = (bf16[1,24576,1,128]{3,1,2,0:T(8,128)(2,1)}, bf16[1,24576,1,128]{3,1,2,0:T(8,128)(2,1)S(1)}, u32[]{:S(2)}) copy-start(bf16[1,24576,1,128]{3,1,2,0:T(8,128)(2,1)S(1)} %get-tuple-element.9) | copy-start | bytes 18874372
where the time goes:
time: 183 us
  blocking collectives  149 us (81%)
  other arithmetic  23.5 us (13%)
  local copies, waits for them, and re-layouts  9.78 us (5%)
    all_to_all x1, blocking collectives, in_one_piece(): lax.all_to_all(both, axis, split_axis=split_dim, concat_axis=concat_dim,...  149 us
    reduce_min x1, other arithmetic, on_device(): page_low = jnp.min(page_view, axis=2)  7.47 us
    concatenate x1, other arithmetic, in_one_piece(): both = jnp.concatenate(arrays, axis=along)  6.43 us
    another operation x1, other arithmetic  5.51 us
    convert_element_type x1, other arithmetic, prepare_keys(): wide_keys = plain_keys.astype(jnp.float32)  4.04 us

commit v1 on v0

v1 whole, which is shorter than its diff:
```python
import jax
import jax.numpy as jnp
from jax import lax
from jax.experimental import pallas as pl
from jax.experimental.pallas import tpu as pltpu
from jax.sharding import PartitionSpec as P

PAGE = 32
SIDE = 4
MESH = pl.DeviceIdType.MESH
FAR_FIRST = (2, 1, 3)


def exchange(keys, values, angles, key_out, value_out, high_out, low_out, raw, turned, relay, angle, cosine, sine,
             tops, bottoms, send_sem, recv_sem, raw_sem, own_sem, angle_sem):
    length = keys.shape[1]
    half = length // 2
    coarse, fine, model = (lax.axis_index(name) for name in ("coarse", "fine", "model"))
    z, y = coarse * 2 + fine // SIDE, fine % SIDE
    me = z * SIDE + y

    def place(dz, dy):
        return (z + dz) % SIDE * SIDE + (y + dy) % SIDE

    def device(dz, dy):
        pz, py = (z + dz) % SIDE, (y + dy) % SIDE
        return (pz // 2, pz % 2 * SIDE + py, model)

    sources = (values, turned)
    outs = (value_out, key_out)

    def ring(way, step):
        return (0, step) if way == 0 else (step, 0)

    def both(way, first, second):
        return (second, first) if way == 0 else (first, second)

    def hop(item, way, leg, first, second):
        rows = pl.ds(way * half, half)
        at = place(*both(way, first, second))
        if leg == 0:
            src = sources[item].at[at, rows]
            if second == 0:
                dst = outs[item].at[me, rows]
            else:
                dst = relay.at[item, way, first - 1, second - 1]
            to = device(*ring(way, first))
        else:
            if first == 0:
                src = sources[item].at[at, rows]
                origin = me
            else:
                src = relay.at[item, way, first - 1, second - 1]
                origin = place(*both(way, -first, 0))
            dst = outs[item].at[origin, rows]
            to = device(*ring(1 - way, second))
        index = ((item * 2 + way) * 2 + leg) * 16 + first * 4 + second
        return pltpu.make_async_remote_copy(
            src_ref=src, dst_ref=dst, send_sem=send_sem.at[index], recv_sem=recv_sem.at[index],
            device_id=to, device_id_type=MESH,
        )

    barrier = pltpu.get_barrier_semaphore()
    for step in (1, 3, 2):
        for way in (0, 1):
            pl.semaphore_signal(barrier, inc=1, device_id=device(*ring(way, step)), device_id_type=MESH)

    columns = pl.ds(pl.multiple_of(me * length, 128), length)
    angle_copy = pltpu.make_async_copy(angles.at[:, columns], angle, angle_sem)
    angle_copy.start()
    raw_copy = [pltpu.make_async_copy(keys.at[b], raw.at[b], raw_sem.at[b]) for b in range(16)]
    for copy in raw_copy:
        copy.start()
    pl.semaphore_wait(barrier, 6)

    started = []

    def start(*which):
        copy = hop(*which)
        copy.start()
        started.append(copy)

    def leave(item):
        for second in (1, 2, 3, 0):
            for first in FAR_FIRST:
                for way in (0, 1):
                    start(item, way, 0, first, second)

    def forward(item):
        for first in (0, 2, 1, 3):
            for second in FAR_FIRST:
                for way in (0, 1):
                    if first:
                        hop(item, way, 0, first, second).wait_recv()
                    start(item, way, 1, first, second)

    leave(0)
    own_value = pltpu.make_async_copy(values.at[me], value_out.at[me], own_sem.at[0])
    own_value.start()

    angle_copy.wait()
    for at in range(0, length, 128):
        block = angle[:, at:at + 128]
        c, s = jnp.cos(block), jnp.sin(block)
        cosine[at:at + 128, :] = jnp.concatenate([c, c], axis=0).T
        sine[at:at + 128, :] = jnp.concatenate([-s, s], axis=0).T

    def turn(b, _):
        pltpu.make_async_copy(keys.at[b], raw.at[b], raw_sem.at[b]).wait()

        def tile(i, _):
            rows = pl.ds(pl.multiple_of(i * 128, 128), 128)
            x = raw[b, rows, :].astype(jnp.float32)
            turned[b, rows, :] = (x * cosine[rows, :] + pltpu.roll(x, 64, 1) * sine[rows, :]).astype(jnp.bfloat16)
            return 0

        return lax.fori_loop(0, length // 128, tile, 0)

    lax.fori_loop(0, 16, turn, 0)
    leave(1)
    own_key = pltpu.make_async_copy(turned.at[me], key_out.at[me], own_sem.at[1])
    own_key.start()
    forward(0)
    forward(1)

    pages = half // PAGE

    def bounds(origin, way):
        base = origin * (2 * pages) + way * pages

        def group(i, _):
            x = key_out[origin, pl.ds(pl.multiple_of(way * half + i * 8 * PAGE, 8 * PAGE), 8 * PAGE), :]
            x = x.astype(jnp.float32).reshape(8, PAGE, x.shape[-1])
            rows = pl.ds(pl.multiple_of(base + i * 8, 8), 8)
            tops[rows, :] = jnp.max(x, axis=1)
            bottoms[rows, :] = jnp.min(x, axis=1)
            return 0

        lax.fori_loop(0, pages // 8, group, 0)

    own_key.wait()
    for way in (0, 1):
        bounds(me, way)
    for first in FAR_FIRST:
        for way in (0, 1):
            hop(1, way, 0, first, 0).wait_recv()
            bounds(place(*both(way, -first, 0)), way)
    for first in (0, 2, 1, 3):
        for second in FAR_FIRST:
            for way in (0, 1):
                hop(1, way, 1, first, second).wait_recv()
                bounds(place(*both(way, -first, -second)), way)
    high_out[...] = tops[...].astype(jnp.bfloat16)
    low_out[...] = bottoms[...].astype(jnp.bfloat16)
    own_value.wait()
    for way in (0, 1):
        for first in FAR_FIRST:
            hop(0, way, 0, first, 0).wait_recv()
        for first in range(4):
            for second in FAR_FIRST:
                hop(0, way, 1, first, second).wait_recv()
    for copy in started:
        copy.wait_send()


def on_device(fresh_keys, fresh_values, turn_angle):
    batch, length, _, size = fresh_keys.shape
    half_head = turn_angle.shape[1]
    pages = batch * length // PAGE
    vmem, any_space = pl.BlockSpec(memory_space=pltpu.VMEM), pl.BlockSpec(memory_space=pl.ANY)
    cache_keys, cache_values, high, low = pl.pallas_call(
        exchange,
        out_shape=(
            pltpu.VMEM((batch, length, size), jnp.bfloat16),
            pltpu.VMEM((batch, length, size), jnp.bfloat16),
            pltpu.VMEM((pages, size), jnp.bfloat16),
            pltpu.VMEM((pages, size), jnp.bfloat16),
        ),
        in_specs=[any_space] * 3,
        out_specs=(vmem,) * 4,
        scratch_shapes=[
            pltpu.VMEM((batch, length, size), jnp.bfloat16),
            pltpu.VMEM((batch, length, size), jnp.bfloat16),
            pltpu.VMEM((2, 2, 3, 3, length // 2, size), jnp.bfloat16),
            pltpu.VMEM((half_head, length), jnp.float32),
            pltpu.VMEM((length, size), jnp.float32),
            pltpu.VMEM((length, size), jnp.float32),
            pltpu.VMEM((pages, size), jnp.float32),
            pltpu.VMEM((pages, size), jnp.float32),
            pltpu.SemaphoreType.DMA((128,)),
            pltpu.SemaphoreType.DMA((128,)),
            pltpu.SemaphoreType.DMA((16,)),
            pltpu.SemaphoreType.DMA((2,)),
            pltpu.SemaphoreType.DMA,
        ],
        compiler_params=pltpu.CompilerParams(
            collective_id=0, has_side_effects=True, vmem_limit_bytes=40 * 2**20
        ),
    )(fresh_keys.reshape(batch, length, size), fresh_values.reshape(batch, length, size), turn_angle.T)
    return (
        cache_keys.reshape(1, -1, 1, size),
        cache_values.reshape(1, -1, 1, size),
        high.reshape(1, -1, 1, size),
        low.reshape(1, -1, 1, size),
    )


def solution(mesh):
    cut = P(None, ("coarse", "fine"), "model", None)
    whole = P(("coarse", "fine"), None, "model", None)
    return jax.shard_map(
        on_device, mesh=mesh, in_specs=(cut, cut, P()), out_specs=(whole,) * 4, check_vma=False
    )
```

time: 183 us -> 154 us (0.84)
  blocking collectives: 149 us -> 0 us
  Pallas kernels: 0 us -> 146 us
  other arithmetic: 23.5 us -> 0 us
  local copies, waits for them, and re-layouts: 9.78 us -> 6.76 us
    all_to_all x1 -> x0, blocking collectives: 149 us -> none  [in_one_piece(): lax.all_to_all(both, axis, split_axis=split_dim, concat_axis=concat_dim,...]
    pallas_call x0 -> x1, Pallas kernels: none -> 146 us  [on_device(): pl.pallas_call(exchange, out_shape=(pltpu.VMEM((batch, length, size), jnp...]
    reduce_min x1 -> x0, other arithmetic: 7.47 us -> none  [on_device(): page_low = jnp.min(page_view, axis=2)]
    unnamed x2 -> x4, local copies, waits for them, and re-layouts: 0.01 us -> 6.76 us
    concatenate x1 -> x0, other arithmetic: 6.43 us -> none  [in_one_piece(): both = jnp.concatenate(arrays, axis=along)]
    another operation x1 -> x0, other arithmetic: 5.51 us -> none
    convert_element_type x1 -> x0, other arithmetic: 4.04 us -> none  [prepare_keys(): wide_keys = plain_keys.astype(jnp.float32)]
    cos x2 -> x0, local copies, waits for them, and re-layouts: 3.49 us -> none  [turn_pairs(): jnp.cos(angle)[None, :, None, :]]
where the time goes in v1:
time: 154 us; the launch traced here: 153 us
  Pallas kernels  146 us (95%)
  local copies, waits for them, and re-layouts  6.76 us (4%)
    pallas_call x1, Pallas kernels, on_device(): pl.pallas_call(exchange, out_shape=(pltpu.VMEM((batch, length, size), jnp...  146 us
    unnamed x4, local copies, waits for them, and re-layouts  6.76 us

profile of v1, /device:TPU:0, one launch (start us, length us, event | category | flops | bytes accessed | tf_op | source)
XLA Modules:
  0.0 153.2 jit_solution(8045164621621736937)
XLA Ops:
  0.6 145.8 %shard_map.66 = (bf16[16,1536,128]{2,1,0:T(8,128)(2,1)S(1)}, bf16[16,1536,128]{2,1,0:T(8,128)(2,1)S(1)}, bf16[768,128]{1,0:T(8,128)(2,1)S(1)}, bf16[768,128]{1,0:T(8,128)(2,1)S(1)}) custom-call(bf16[16,1536,128]{2,1,0:T(8,128)(2,1)} %bitcast.11, bf16[16,1536,128]{2,1,0:T(8,128)(2,1)} %bitcast.12, f32[64,24576]{1,0:T(8,128)} %bitcast.13), custom_call_target="tpu_custom_call" | custom-call | tf_op jit(solution)/shard_map/pallas_call | solution.py:171
  146.5 2.7 %copy.11 = bf16[1,24576,1,128]{3,1,2,0:T(8,128)(2,1)} copy(bf16[1,24576,1,128]{3,1,2,0:T(8,128)(2,1)S(1)} %bitcast.8) | data formatting | bytes 12582912
  149.2 2.7 %copy.12 = bf16[1,24576,1,128]{3,1,2,0:T(8,128)(2,1)} copy(bf16[1,24576,1,128]{3,1,2,0:T(8,128)(2,1)S(1)} %bitcast.7) | data formatting | bytes 12582912
  151.9 0.7 copy.13
  152.6 0.7 copy.14

commit v2 on v1

--- a/solution.py
+++ b/solution.py
@@ -163,6 +163,21 @@
         copy.wait_send()
 
 
+def write_out(*refs):
+    count = (len(refs) - 1) // 2
+    sems, copies = refs[-1], []
+    for i in range(count):
+        src, dst = refs[i], refs[count + i]
+        parts = 4 if len(src.shape) == 3 else 1
+        size = src.shape[0] // parts
+        for part in range(parts):
+            at = pl.ds(part * size, size)
+            copies.append(pltpu.make_async_copy(src.at[at], dst.at[at], sems.at[len(copies)]))
+            copies[-1].start()
+    for copy in copies:
+        copy.wait()
+
+
 def on_device(fresh_keys, fresh_values, turn_angle):
     batch, length, _, size = fresh_keys.shape
     half_head = turn_angle.shape[1]
@@ -197,6 +212,15 @@
             collective_id=0, has_side_effects=True, vmem_limit_bytes=40 * 2**20
         ),
     )(fresh_keys.reshape(batch, length, size), fresh_values.reshape(batch, length, size), turn_angle.T)
+    moved = (cache_keys, cache_values, high, low)
+    cache_keys, cache_values, high, low = pl.pallas_call(
+        write_out,
+        out_shape=tuple(jax.ShapeDtypeStruct(x.shape, x.dtype) for x in moved),
+        in_specs=[vmem] * 4,
+        out_specs=(any_space,) * 4,
+        scratch_shapes=[pltpu.SemaphoreType.DMA((10,))],
+        compiler_params=pltpu.CompilerParams(vmem_limit_bytes=2**20),
+    )(*moved)
     return (
         cache_keys.reshape(1, -1, 1, size),
         cache_values.reshape(1, -1, 1, size),

time: 154 us -> 152 us (0.987)
  local copies, waits for them, and re-layouts: 6.76 us -> 0 us
  Pallas kernels: 146 us -> 151 us
    unnamed x4 -> x0, local copies, waits for them, and re-layouts: 6.76 us -> none
    pallas_call x0 -> x1, Pallas kernels: none -> 4.74 us  [on_device(): pl.pallas_call(write_out, out_shape=tuple((jax.ShapeDtypeStruct(x.shape,...]
where the time goes in v2:
time: 152 us; the launch traced here: 151 us
  Pallas kernels  151 us (99%)
    pallas_call x1, Pallas kernels, on_device(): pl.pallas_call(exchange, out_shape=(pltpu.VMEM((batch, length, size), jnp...  146 us
    pallas_call x1, Pallas kernels, on_device(): pl.pallas_call(write_out, out_shape=tuple((jax.ShapeDtypeStruct(x.shape,...  4.74 us

profile of v2, /device:TPU:0, one launch (start us, length us, event | category | flops | bytes accessed | tf_op | source)
XLA Modules:
  0.0 151.2 jit_solution(8847136709432099291)
XLA Ops:
  0.6 145.8 %shard_map.66 = (bf16[16,1536,128]{2,1,0:T(8,128)(2,1)S(1)}, bf16[16,1536,128]{2,1,0:T(8,128)(2,1)S(1)}, bf16[768,128]{1,0:T(8,128)(2,1)S(1)}, bf16[768,128]{1,0:T(8,128)(2,1)S(1)}) custom-call(bf16[16,1536,128]{2,1,0:T(8,128)(2,1)} %bitcast.7, bf16[16,1536,128]{2,1,0:T(8,128)(2,1)} %bitcast.8, f32[64,24576]{1,0:T(8,128)} %bitcast.9), custom_call_target="tpu_custom_call" | custom-call | tf_op jit(solution)/shard_map/pallas_call | solution.py:186
  146.5 4.7 %shard_map.67 = (bf16[16,1536,128]{2,1,0:T(8,128)(2,1)}, bf16[16,1536,128]{2,1,0:T(8,128)(2,1)}, bf16[768,128]{1,0:T(8,128)(2,1)}, bf16[768,128]{1,0:T(8,128)(2,1)}) custom-call(bf16[16,1536,128]{2,1,0:T(8,128)(2,1)S(1)} %get-tuple-element.12.refs_0_, bf16[16,1536,128]{2,1,0:T(8,128)(2,1)S(1)} %get-tuple-element.13.refs_1_, ...), custom_call_target="tpu_custom_call" | custom-call | tf_op jit(solution)/shard_map/pallas_call | solution.py:216

commit v3 on v2

--- a/solution.py
+++ b/solution.py
@@ -12,7 +12,7 @@
 
 
 def exchange(keys, values, angles, key_out, value_out, high_out, low_out, raw, turned, relay, angle, cosine, sine,
-             tops, bottoms, send_sem, recv_sem, raw_sem, own_sem, angle_sem):
+             tops, bottoms, send_sem, recv_sem, raw_sem, own_sem, angle_sem, ready):
     length = keys.shape[1]
     half = length // 2
     coarse, fine, model = (lax.axis_index(name) for name in ("coarse", "fine", "model"))
@@ -22,9 +22,9 @@
     def place(dz, dy):
         return (z + dz) % SIDE * SIDE + (y + dy) % SIDE
 
-    def device(dz, dy):
+    def device(dz, dy, at=model):
         pz, py = (z + dz) % SIDE, (y + dy) % SIDE
-        return (pz // 2, pz % 2 * SIDE + py, model)
+        return (pz // 2, pz % 2 * SIDE + py, at)
 
     sources = (values, turned)
     outs = (value_out, key_out)
@@ -60,10 +60,14 @@
             device_id=to, device_id_type=MESH,
         )
 
+    core = model % 2
+    partner = (coarse, fine, model + 1 - 2 * core)
     barrier = pltpu.get_barrier_semaphore()
     for step in (1, 3, 2):
         for way in (0, 1):
-            pl.semaphore_signal(barrier, inc=1, device_id=device(*ring(way, step)), device_id_type=MESH)
+            gatherer = device(*ring(way, step), model - core + way)
+            pl.semaphore_signal(barrier, inc=1, device_id=gatherer, device_id_type=MESH)
+    pl.semaphore_signal(barrier, inc=1, device_id=partner, device_id_type=MESH)
 
     columns = pl.ds(pl.multiple_of(me * length, 128), length)
     angle_copy = pltpu.make_async_copy(angles.at[:, columns], angle, angle_sem)
@@ -71,19 +75,19 @@
     raw_copy = [pltpu.make_async_copy(keys.at[b], raw.at[b], raw_sem.at[b]) for b in range(16)]
     for copy in raw_copy:
         copy.start()
-    pl.semaphore_wait(barrier, 6)
+    pl.semaphore_wait(barrier, 7)
+    pl.semaphore_signal(ready, inc=1, device_id=partner, device_id_type=MESH)
 
     started = []
 
     def start(*which):
-        copy = hop(*which)
-        copy.start()
-        started.append(copy)
-
-    def leave(item):
+        hop(*which).start()
+        started.append(which)
+
+    def leave(item, ways):
         for second in (1, 2, 3, 0):
             for first in FAR_FIRST:
-                for way in (0, 1):
+                for way in ways:
                     start(item, way, 0, first, second)
 
     def forward(item):
@@ -94,7 +98,14 @@
                         hop(item, way, 0, first, second).wait_recv()
                     start(item, way, 1, first, second)
 
-    leave(0)
+    for mine in (0, 1):
+
+        @pl.when(core == mine)
+        def _():
+            leave(0, (mine,))
+            pl.semaphore_wait(ready, 1)
+            leave(0, (1 - mine,))
+
     own_value = pltpu.make_async_copy(values.at[me], value_out.at[me], own_sem.at[0])
     own_value.start()
 
@@ -117,11 +128,11 @@
         return lax.fori_loop(0, length // 128, tile, 0)
 
     lax.fori_loop(0, 16, turn, 0)
-    leave(1)
+    leave(1, (0, 1))
     own_key = pltpu.make_async_copy(turned.at[me], key_out.at[me], own_sem.at[1])
     own_key.start()
+    forward(1)
     forward(0)
-    forward(1)
 
     pages = half // PAGE
 
@@ -159,8 +170,8 @@
         for first in range(4):
             for second in FAR_FIRST:
                 hop(0, way, 1, first, second).wait_recv()
-    for copy in started:
-        copy.wait_send()
+    for which in sorted(set(started)):
+        hop(*which).wait_send()
 
 
 def write_out(*refs):
@@ -207,6 +218,7 @@
             pltpu.SemaphoreType.DMA((16,)),
             pltpu.SemaphoreType.DMA((2,)),
             pltpu.SemaphoreType.DMA,
+            pltpu.SemaphoreType.REGULAR,
         ],
         compiler_params=pltpu.CompilerParams(
             collective_id=0, has_side_effects=True, vmem_limit_bytes=40 * 2**20

time: 152 us -> 150 us (0.987)
  Pallas kernels: 151 us -> 149 us
where the time goes in v3:
time: 150 us
  Pallas kernels  149 us (99%)
    pallas_call x1, Pallas kernels, on_device(): pl.pallas_call(exchange, out_shape=(pltpu.VMEM((batch, length, size), jnp...  144 us
    pallas_call x1, Pallas kernels, on_device(): pl.pallas_call(write_out, out_shape=tuple((jax.ShapeDtypeStruct(x.shape,...  4.74 us

profile of v3, /device:TPU:0, one launch (start us, length us, event | category | flops | bytes accessed | tf_op | source)
XLA Modules:
  0.0 149.8 jit_solution(12572566441175634382)
XLA Ops:
  0.6 144.5 %shard_map.66 = (bf16[16,1536,128]{2,1,0:T(8,128)(2,1)S(1)}, bf16[16,1536,128]{2,1,0:T(8,128)(2,1)S(1)}, bf16[768,128]{1,0:T(8,128)(2,1)S(1)}, bf16[768,128]{1,0:T(8,128)(2,1)S(1)}) custom-call(bf16[16,1536,128]{2,1,0:T(8,128)(2,1)} %bitcast.7, bf16[16,1536,128]{2,1,0:T(8,128)(2,1)} %bitcast.8, f32[64,24576]{1,0:T(8,128)} %bitcast.9), custom_call_target="tpu_custom_call" | custom-call | tf_op jit(solution)/shard_map/pallas_call | solution.py:197
  145.1 4.7 %shard_map.67 = (bf16[16,1536,128]{2,1,0:T(8,128)(2,1)}, bf16[16,1536,128]{2,1,0:T(8,128)(2,1)}, bf16[768,128]{1,0:T(8,128)(2,1)}, bf16[768,128]{1,0:T(8,128)(2,1)}) custom-call(bf16[16,1536,128]{2,1,0:T(8,128)(2,1)S(1)} %get-tuple-element.12.refs_0_, bf16[16,1536,128]{2,1,0:T(8,128)(2,1)S(1)} %get-tuple-element.13.refs_1_, ...), custom_call_target="tpu_custom_call" | custom-call | tf_op jit(solution)/shard_map/pallas_call | solution.py:228

commit v4 on v3

v4 whole, which is shorter than its diff:
```python
import types

import jax
import jax.numpy as jnp
from jax import lax
from jax.experimental import pallas as pl
from jax.experimental.pallas import tpu as pltpu
from jax.sharding import PartitionSpec as P

PAGE = 32
SIDE = 4
MESH = pl.DeviceIdType.MESH
FAR_FIRST = (2, 1, 3)
GROUPS = (0, 2, 1, 3)
LATE = ((0, 1, 2, 3), ())


def layout(length):
    half = length // 2
    coarse, fine, model = (lax.axis_index(name) for name in ("coarse", "fine", "model"))
    z, y = coarse * 2 + fine // SIDE, fine % SIDE

    def place(dz, dy):
        return (z + dz) % SIDE * SIDE + (y + dy) % SIDE

    def device(dz, dy, at=model):
        pz, py = (z + dz) % SIDE, (y + dy) % SIDE
        return (pz // 2, pz % 2 * SIDE + py, at)

    def ring(way, step):
        return (0, step) if way == 0 else (step, 0)

    def both(way, first, second):
        return (second, first) if way == 0 else (first, second)

    def rows(way):
        return pl.ds(way * half, half)

    core = model % 2

    def on_late(first, late, body):
        cores = [c for c in (0, 1) if (first in LATE[c]) == late]
        if len(cores) == 2:
            body()
        elif cores:
            pl.when(core == cores[0])(body)

    return types.SimpleNamespace(
        half=half, coarse=coarse, model=model, fine=fine, me=z * SIDE + y, core=core, place=place, device=device,
        ring=ring, both=both, rows=rows, on_late=on_late,
    )


def page_bounds(keys, origin, way, tops, bottoms):
    half = keys.shape[1] // 2
    pages = half // PAGE
    base = origin * (2 * pages) + way * pages

    def group(i, _):
        x = keys[origin, pl.ds(pl.multiple_of(way * half + i * 8 * PAGE, 8 * PAGE), 8 * PAGE), :]
        x = x.astype(jnp.float32).reshape(8, PAGE, x.shape[-1])
        rows = pl.ds(pl.multiple_of(base + i * 8, 8), 8)
        tops[rows, :] = jnp.max(x, axis=1)
        bottoms[rows, :] = jnp.min(x, axis=1)
        return 0

    lax.fori_loop(0, pages // 8, group, 0)


def exchange(keys, values, angles, key_out, value_out, key_relay, tops, bottoms, raw, turned, value_relay, angle,
             cosine, sine, send_sem, recv_sem, raw_sem, own_sem, angle_sem, keep_sem, ready):
    length = keys.shape[1]
    at = layout(length)
    me, core, place, device, ring, both = at.me, at.core, at.place, at.device, at.ring, at.both
    sources = (values, turned)
    outs = (value_out, key_out)
    relays = (value_relay, key_relay)

    def hop(item, way, leg, first, second):
        rows = at.rows(way)
        goal = place(*both(way, first, second))
        if leg == 0:
            src = sources[item].at[goal, rows]
            if second == 0:
                dst = outs[item].at[me, rows]
            else:
                dst = relays[item].at[way, first, second - 1]
            to = device(*ring(way, first))
        else:
            if first == 0:
                src = sources[item].at[goal, rows]
                origin = me
            else:
                src = relays[item].at[way, first, second - 1]
                origin = place(*both(way, -first, 0))
            dst = outs[item].at[origin, rows]
            to = device(*ring(1 - way, second))
        index = ((item * 2 + way) * 2 + leg) * 16 + first * 4 + second
        return pltpu.make_async_remote_copy(
            src_ref=src, dst_ref=dst, send_sem=send_sem.at[index], recv_sem=recv_sem.at[index],
            device_id=to, device_id_type=MESH,
        )

    partner = (at.coarse, at.fine, at.model + 1 - 2 * core)
    barrier = pltpu.get_barrier_semaphore()
    for step in (1, 3, 2):
        for way in (0, 1):
            gatherer = device(*ring(way, step), at.model - core + way)
            pl.semaphore_signal(barrier, inc=1, device_id=gatherer, device_id_type=MESH)
    pl.semaphore_signal(barrier, inc=1, device_id=partner, device_id_type=MESH)

    columns = pl.ds(pl.multiple_of(me * length, 128), length)
    angle_copy = pltpu.make_async_copy(angles.at[:, columns], angle, angle_sem)
    angle_copy.start()
    for b in range(16):
        pltpu.make_async_copy(keys.at[b], raw.at[b], raw_sem.at[b]).start()
    pl.semaphore_wait(barrier, 7)
    pl.semaphore_signal(ready, inc=1, device_id=partner, device_id_type=MESH)

    def leave(item, ways):
        for second in (1, 2, 3, 0):
            for first in FAR_FIRST:
                for way in ways:
                    hop(item, way, 0, first, second).start()

    def forward(item, first):
        for second in FAR_FIRST:
            for way in (0, 1):
                if first:
                    hop(item, way, 0, first, second).wait_recv()
                hop(item, way, 1, first, second).start()

    for mine in (0, 1):

        @pl.when(core == mine)
        def _():
            leave(0, (mine,))
            pl.semaphore_wait(ready, 1)
            leave(0, (1 - mine,))

    own_value = pltpu.make_async_copy(values.at[me], value_out.at[me], own_sem.at[0])
    own_value.start()

    angle_copy.wait()
    for start in range(0, length, 128):
        block = angle[:, start:start + 128]
        c, s = jnp.cos(block), jnp.sin(block)
        cosine[start:start + 128, :] = jnp.concatenate([c, c], axis=0).T
        sine[start:start + 128, :] = jnp.concatenate([-s, s], axis=0).T

    def turn(b, _):
        pltpu.make_async_copy(keys.at[b], raw.at[b], raw_sem.at[b]).wait()

        def tile(i, _):
            rows = pl.ds(pl.multiple_of(i * 128, 128), 128)
            x = raw[b, rows, :].astype(jnp.float32)
            turned[b, rows, :] = (x * cosine[rows, :] + pltpu.roll(x, 64, 1) * sine[rows, :]).astype(jnp.bfloat16)
            return 0

        return lax.fori_loop(0, length // 128, tile, 0)

    lax.fori_loop(0, 16, turn, 0)
    leave(1, (0, 1))
    own_key = pltpu.make_async_copy(turned.at[me], key_out.at[me], own_sem.at[1])
    own_key.start()
    for first in GROUPS:
        at.on_late(first, False, lambda: forward(1, first))
    for first in GROUPS:
        forward(0, first)

    def keep(way, second):
        index = way * 3 + second - 1
        return pltpu.make_async_copy(
            turned.at[place(*both(way, 0, second)), at.rows(way)], key_relay.at[way, 0, second - 1], keep_sem.at[index]
        )

    def relayed(first):
        for second in FAR_FIRST:
            for way in (0, 1):
                if first:
                    hop(1, way, 0, first, second).wait_recv()
                else:
                    keep(way, second).wait()

    for way in (0, 1):
        for second in FAR_FIRST:
            at.on_late(0, True, lambda: keep(way, second).start())

    own_key.wait()
    for way in (0, 1):
        page_bounds(key_out, me, way, tops, bottoms)
    for first in FAR_FIRST:
        for way in (0, 1):
            hop(1, way, 0, first, 0).wait_recv()
            page_bounds(key_out, place(*both(way, -first, 0)), way, tops, bottoms)

    def arrive(first):
        for second in FAR_FIRST:
            for way in (0, 1):
                hop(1, way, 1, first, second).wait_recv()
                page_bounds(key_out, place(*both(way, -first, -second)), way, tops, bottoms)

    for first in GROUPS:
        at.on_late(first, False, lambda: arrive(first))
        at.on_late(first, True, lambda: relayed(first))
    own_value.wait()

    def left(item, first):
        for second in FAR_FIRST:
            for way in (0, 1):
                hop(item, way, 1, first, second).wait_send()

    for way in (0, 1):
        for first in FAR_FIRST:
            hop(0, way, 0, first, 0).wait_recv()
            for second in range(4):
                hop(0, way, 0, first, second).wait_send()
                hop(1, way, 0, first, second).wait_send()
        for first in range(4):
            for second in FAR_FIRST:
                hop(0, way, 1, first, second).wait_recv()
    for first in range(4):
        left(0, first)
        at.on_late(first, False, lambda: left(1, first))


def last_groups(relay, early_tops, early_bottoms, _, key_out, high_out, low_out, tops, bottoms, send_sem, recv_sem):
    at = layout(key_out.shape[1])
    place, both = at.place, at.both

    def hop(way, first, second):
        index = (way * 4 + first) * 4 + second
        return pltpu.make_async_remote_copy(
            src_ref=relay.at[way, first, second - 1],
            dst_ref=key_out.at[place(*both(way, -first, 0)), at.rows(way)],
            send_sem=send_sem.at[index], recv_sem=recv_sem.at[index],
            device_id=at.device(*at.ring(1 - way, second)), device_id_type=MESH,
        )

    barrier = pltpu.get_barrier_semaphore()
    for step in (1, 3, 2):
        for way in (0, 1):
            pl.semaphore_signal(barrier, inc=1, device_id=at.device(*at.ring(way, step)), device_id_type=MESH)
    pl.semaphore_wait(barrier, 6)

    def start(first):
        for second in FAR_FIRST:
            for way in (0, 1):
                hop(way, first, second).start()

    def arrive(first):
        for second in FAR_FIRST:
            for way in (0, 1):
                hop(way, first, second).wait_recv()
                page_bounds(key_out, place(*both(way, -first, -second)), way, tops, bottoms)

    def left(first):
        for second in FAR_FIRST:
            for way in (0, 1):
                hop(way, first, second).wait_send()

    for first in GROUPS:
        at.on_late(first, True, lambda: start(first))
    tops[...] = early_tops[...]
    bottoms[...] = early_bottoms[...]
    for first in GROUPS:
        at.on_late(first, True, lambda: arrive(first))
    high_out[...] = tops[...].astype(jnp.bfloat16)
    low_out[...] = bottoms[...].astype(jnp.bfloat16)
    for first in GROUPS:
        at.on_late(first, True, lambda: left(first))


def write_early(key_in, value_in, key_out, value_out, done, sems):
    at = layout(key_in.shape[1])

    def value_part(part):
        rows = pl.ds(part * 4, 4)
        return pltpu.make_async_copy(value_in.at[rows], value_out.at[rows], sems.at[part])

    def key_part(way, first, second):
        here = (at.place(*at.both(way, -first, -second)), at.rows(way))
        return pltpu.make_async_copy(key_in.at[here], key_out.at[here], sems.at[4 + (way * 4 + first) * 4 + second])

    def steps(first):
        return FAR_FIRST + (0,)

    def start(first):
        for second in steps(first):
            for way in (0, 1):
                key_part(way, first, second).start()

    def wait(first):
        for second in steps(first):
            for way in (0, 1):
                key_part(way, first, second).wait()

    def direct(first, act):
        for way in (0, 1):
            act(key_part(way, first, 0))

    done[...] = jnp.zeros_like(done)
    for part in range(4):
        value_part(part).start()
    for first in GROUPS:
        at.on_late(first, True, lambda: direct(first, lambda copy: copy.start()))
        at.on_late(first, False, lambda: start(first))
    for part in range(4):
        value_part(part).wait()
    for first in GROUPS:
        at.on_late(first, True, lambda: direct(first, lambda copy: copy.wait()))
        at.on_late(first, False, lambda: wait(first))


def write_late(_, key_in, high_in, low_in, key_out, high_out, low_out, sems):
    at = layout(key_in.shape[1])

    def key_part(way, first, second):
        here = (at.place(*at.both(way, -first, -second)), at.rows(way))
        return pltpu.make_async_copy(key_in.at[here], key_out.at[here], sems.at[(way * 4 + first) * 4 + second])

    def start(first):
        for second in FAR_FIRST:
            for way in (0, 1):
                key_part(way, first, second).start()

    def wait(first):
        for second in FAR_FIRST:
            for way in (0, 1):
                key_part(way, first, second).wait()

    high = pltpu.make_async_copy(high_in, high_out, sems.at[0])
    low = pltpu.make_async_copy(low_in, low_out, sems.at[16])
    high.start()
    low.start()
    for first in GROUPS:
        at.on_late(first, True, lambda: start(first))
    high.wait()
    low.wait()
    for first in GROUPS:
        at.on_late(first, True, lambda: wait(first))


def on_device(fresh_keys, fresh_values, turn_angle):
    batch, length, _, size = fresh_keys.shape
    half_head = turn_angle.shape[1]
    pages = batch * length // PAGE
    vmem, any_space = pl.BlockSpec(memory_space=pltpu.VMEM), pl.BlockSpec(memory_space=pl.ANY)
    whole, relay = (batch, length, size), (2, SIDE, SIDE - 1, length // 2, size)
    early_keys, early_values, key_relay, tops, bottoms = pl.pallas_call(
        exchange,
        out_shape=(
            pltpu.VMEM(whole, jnp.bfloat16),
            pltpu.VMEM(whole, jnp.bfloat16),
            pltpu.VMEM(relay, jnp.bfloat16),
            pltpu.VMEM((pages, size), jnp.float32),
            pltpu.VMEM((pages, size), jnp.float32),
        ),
        in_specs=[any_space] * 3,
        out_specs=(vmem,) * 5,
        scratch_shapes=[
            pltpu.VMEM(whole, jnp.bfloat16),
            pltpu.VMEM(whole, jnp.bfloat16),
            pltpu.VMEM(relay, jnp.bfloat16),
            pltpu.VMEM((half_head, length), jnp.float32),
            pltpu.VMEM((length, size), jnp.float32),
            pltpu.VMEM((length, size), jnp.float32),
            pltpu.SemaphoreType.DMA((128,)),
            pltpu.SemaphoreType.DMA((128,)),
            pltpu.SemaphoreType.DMA((16,)),
            pltpu.SemaphoreType.DMA((2,)),
            pltpu.SemaphoreType.DMA,
            pltpu.SemaphoreType.DMA((6,)),
            pltpu.SemaphoreType.REGULAR,
        ],
        compiler_params=pltpu.CompilerParams(
            collective_id=0, has_side_effects=True, vmem_limit_bytes=43 * 2**20
        ),
    )(fresh_keys.reshape(whole), fresh_values.reshape(whole), turn_angle.T)
    some_keys, cache_values, written = pl.pallas_call(
        write_early,
        out_shape=(jax.ShapeDtypeStruct(whole, jnp.bfloat16),) * 2 + (pltpu.VMEM((8, size), jnp.float32),),
        in_specs=[vmem] * 2,
        out_specs=(any_space, any_space, vmem),
        scratch_shapes=[pltpu.SemaphoreType.DMA((36,))],
        compiler_params=pltpu.CompilerParams(vmem_limit_bytes=2**20),
    )(early_keys, early_values)
    late_keys, high, low = pl.pallas_call(
        last_groups,
        out_shape=(
            pltpu.VMEM(whole, jnp.bfloat16),
            pltpu.VMEM((pages, size), jnp.bfloat16),
            pltpu.VMEM((pages, size), jnp.bfloat16),
        ),
        in_specs=[vmem] * 4,
        out_specs=(vmem,) * 3,
        scratch_shapes=[
            pltpu.VMEM((pages, size), jnp.float32),
            pltpu.VMEM((pages, size), jnp.float32),
            pltpu.SemaphoreType.DMA((32,)),
            pltpu.SemaphoreType.DMA((32,)),
        ],
        compiler_params=pltpu.CompilerParams(
            collective_id=1, has_side_effects=True, vmem_limit_bytes=4 * 2**20
        ),
    )(key_relay, tops, bottoms, written)
    cache_keys, high, low = pl.pallas_call(
        write_late,
        out_shape=(
            jax.ShapeDtypeStruct(whole, jnp.bfloat16),
            jax.ShapeDtypeStruct((pages, size), jnp.bfloat16),
            jax.ShapeDtypeStruct((pages, size), jnp.bfloat16),
        ),
        in_specs=[any_space] + [vmem] * 3,
        out_specs=(any_space,) * 3,
        input_output_aliases={0: 0},
        scratch_shapes=[pltpu.SemaphoreType.DMA((32,))],
        compiler_params=pltpu.CompilerParams(vmem_limit_bytes=2**20),
    )(some_keys, late_keys, high, low)
    return (
        cache_keys.reshape(1, -1, 1, size),
        cache_values.reshape(1, -1, 1, size),
        high.reshape(1, -1, 1, size),
        low.reshape(1, -1, 1, size),
    )


def solution(mesh):
    cut = P(None, ("coarse", "fine"), "model", None)
    whole = P(("coarse", "fine"), None, "model", None)
    return jax.shard_map(
        on_device, mesh=mesh, in_specs=(cut, cut, P()), out_specs=(whole,) * 4, check_vma=False
    )
```

time: 150 us -> 146 us (0.973)
  Pallas kernels: 149 us -> 145 us
    pallas_call x2 -> x4, Pallas kernels: 149 us -> 145 us  [the longest x1 113 us: on_device(): pl.pallas_call(exchange, out_shape=(pltpu.VMEM(whole, jnp.bfloat16), pltp...]
where the time goes in v4:
time: 146 us
  Pallas kernels  145 us (99%)
    pallas_call x1, Pallas kernels, on_device(): pl.pallas_call(exchange, out_shape=(pltpu.VMEM(whole, jnp.bfloat16), pltp...  113 us
    pallas_call x1, Pallas kernels, on_device(): pl.pallas_call(last_groups, out_shape=(pltpu.VMEM(whole, jnp.bfloat16), p...  26.5 us
    pallas_call x1, Pallas kernels, on_device(): pl.pallas_call(write_early, out_shape=(jax.ShapeDtypeStruct(whole, jnp.bf...  3.44 us

profile of v4, /device:TPU:0, one launch (start us, length us, event | category | flops | bytes accessed | tf_op | source)
XLA Modules:
  0.0 146.0 jit_solution(11518597648407117360)
XLA Ops:
  0.6 112.9 %shard_map.66 = (bf16[16,1536,128]{2,1,0:T(8,128)(2,1)S(1)}, bf16[16,1536,128]{2,1,0:T(8,128)(2,1)S(1)}, bf16[2,4,3,768,128]{4,3,2,1,0:T(8,128)(2,1)S(1)}, f32[768,128]{1,0:T(8,128)S(1)}, f32[768,128]{1,0:T(8,128)S(1)}) custom-call(bf16[16,1536,128]{2,1,0:T(8,128)(2,1)} %bitcast.8, bf16[16,1536,128]{2,1,0:T(8,128)(2,1)} %bitcast.9, f32[64,24576]{1,0:T(8,128)} %bitcast.10), custom_call_target="tpu_custom_call" | custom-call | tf_op jit(solution)/shard_map/pallas_call | solution.py:350
  113.5 3.4 %shard_map.67 = (bf16[16,1536,128]{2,1,0:T(8,128)(2,1)}, bf16[16,1536,128]{2,1,0:T(8,128)(2,1)}, f32[8,128]{1,0:T(8,128)S(1)}) custom-call(bf16[16,1536,128]{2,1,0:T(8,128)(2,1)S(1)} %get-tuple-element.18.key_in, bf16[16,1536,128]{2,1,0:T(8,128)(2,1)S(1)} %get-tuple-element.19.value_in), custom_call_target="tpu_custom_call" | custom-call | tf_op jit(solution)/shard_map/pallas_call | solution.py:380
  116.9 26.5 %shard_map.68 = (bf16[16,1536,128]{2,1,0:T(8,128)(2,1)S(1)}, bf16[768,128]{1,0:T(8,128)(2,1)S(1)}, bf16[768,128]{1,0:T(8,128)(2,1)S(1)}) custom-call(bf16[2,4,3,768,128]{4,3,2,1,0:T(8,128)(2,1)S(1)} %get-tuple-element.21.relay, f32[768,128]{1,0:T(8,128)S(1)} %get-tuple-element.22.early_tops, f32[768,128]{1,0:T(8,128)S(1)} %get-tuple-element.23.early_bottoms, ...), custom_call_target="tpu_custom_call" | custom-call | tf_op jit(solution)/shard_map/pallas_call | solution.py:388
  143.4 2.6 %shard_map.69 = (bf16[16,1536,128]{2,1,0:T(8,128)(2,1)}, bf16[768,128]{1,0:T(8,128)(2,1)}, bf16[768,128]{1,0:T(8,128)(2,1)}) custom-call(bf16[16,1536,128]{2,1,0:T(8,128)(2,1)} %get-tuple-element.20._, bf16[16,1536,128]{2,1,0:T(8,128)(2,1)S(1)} %get-tuple-element.25.key_in, ...), custom_call_target="tpu_custom_call", output_to_operand_aliasing={{0}: (0, {})} | custom-call | tf_op jit(solution)/shard_map/pallas_call | solution.py:407

commit v5 on v4

v5 whole, which is shorter than its diff:
```python
import types

import jax
import jax.numpy as jnp
from jax import lax
from jax.experimental import pallas as pl
from jax.experimental.pallas import tpu as pltpu
from jax.sharding import PartitionSpec as P

PAGE = 32
SIDE = 4
MESH = pl.DeviceIdType.MESH
FAR_FIRST = (2, 1, 3)
GROUPS = (0, 2, 1, 3)
LATE = (1, 2, 3)


def layout(length):
    half = length // 2
    coarse, fine, model = (lax.axis_index(name) for name in ("coarse", "fine", "model"))
    z, y = coarse * 2 + fine // SIDE, fine % SIDE

    def place(dz, dy):
        return (z + dz) % SIDE * SIDE + (y + dy) % SIDE

    def device(dz, dy, at=model):
        pz, py = (z + dz) % SIDE, (y + dy) % SIDE
        return (pz // 2, pz % 2 * SIDE + py, at)

    def ring(way, step):
        return (0, step) if way == 0 else (step, 0)

    def both(way, first, second):
        return (second, first) if way == 0 else (first, second)

    def rows(way):
        return pl.ds(way * half, half)

    core = model % 2

    def on_late(first, late, body):
        if first not in LATE:
            if not late:
                body()
        else:
            pl.when(core == (0 if late else 1))(body)

    return types.SimpleNamespace(
        half=half, coarse=coarse, model=model, fine=fine, me=z * SIDE + y, core=core, place=place, device=device,
        ring=ring, both=both, rows=rows, on_late=on_late,
    )


def page_bounds(keys, origin, way, tops, bottoms):
    half = keys.shape[1] // 2
    pages = half // PAGE
    base = origin * (2 * pages) + way * pages

    def group(i, _):
        x = keys[origin, pl.ds(pl.multiple_of(way * half + i * 8 * PAGE, 8 * PAGE), 8 * PAGE), :]
        x = x.astype(jnp.float32).reshape(8, PAGE, x.shape[-1])
        rows = pl.ds(pl.multiple_of(base + i * 8, 8), 8)
        tops[rows, :] = jnp.max(x, axis=1)
        bottoms[rows, :] = jnp.min(x, axis=1)
        return 0

    lax.fori_loop(0, pages // 8, group, 0)


def exchange(keys, values, angles, key_out, value_out, value_relay, high_out, low_out, raw, turned, key_relay, tops,
             bottoms, angle, cosine, sine, send_sem, recv_sem, raw_sem, own_sem, angle_sem, keep_sem, ready):
    length = keys.shape[1]
    at = layout(length)
    me, core, place, device, ring, both = at.me, at.core, at.place, at.device, at.ring, at.both
    sources = (values, turned)
    outs = (value_out, key_out)

    def held(item, way, first, second):
        if item:
            return key_relay.at[way, first - 1, second - 1]
        return value_relay.at[way, first, second - 1]

    def hop(item, way, leg, first, second):
        rows = at.rows(way)
        goal = place(*both(way, first, second))
        if leg == 0:
            src = sources[item].at[goal, rows]
            if second == 0:
                dst = outs[item].at[me, rows]
            else:
                dst = held(item, way, first, second)
            to = device(*ring(way, first))
        else:
            if first == 0:
                src = sources[item].at[goal, rows]
                origin = me
            else:
                src = held(item, way, first, second)
                origin = place(*both(way, -first, 0))
            dst = outs[item].at[origin, rows]
            to = device(*ring(1 - way, second))
        index = ((item * 2 + way) * 2 + leg) * 16 + first * 4 + second
        return pltpu.make_async_remote_copy(
            src_ref=src, dst_ref=dst, send_sem=send_sem.at[index], recv_sem=recv_sem.at[index],
            device_id=to, device_id_type=MESH,
        )

    partner = (at.coarse, at.fine, at.model + 1 - 2 * core)
    barrier = pltpu.get_barrier_semaphore()
    for step in (1, 3, 2):
        for way in (0, 1):
            gatherer = device(*ring(way, step), at.model - core + way)
            pl.semaphore_signal(barrier, inc=1, device_id=gatherer, device_id_type=MESH)
    pl.semaphore_signal(barrier, inc=1, device_id=partner, device_id_type=MESH)

    columns = pl.ds(pl.multiple_of(me * length, 128), length)
    angle_copy = pltpu.make_async_copy(angles.at[:, columns], angle, angle_sem)
    angle_copy.start()
    for b in range(16):
        pltpu.make_async_copy(keys.at[b], raw.at[b], raw_sem.at[b]).start()
    pl.semaphore_wait(barrier, 7)
    pl.semaphore_signal(ready, inc=1, device_id=partner, device_id_type=MESH)

    def leave(item, ways):
        for second in (1, 2, 3, 0):
            for first in FAR_FIRST:
                for way in ways:
                    hop(item, way, 0, first, second).start()

    def forward(item, first):
        for second in FAR_FIRST:
            for way in (0, 1):
                if first:
                    hop(item, way, 0, first, second).wait_recv()
                hop(item, way, 1, first, second).start()

    def sent(item, leg):
        for way in (0, 1):
            for first in range(1 - leg, 4):
                for second in FAR_FIRST if leg else range(4):
                    hop(item, way, leg, first, second).wait_send()

    def hold(item, leg):
        pl.when(core == 1)(lambda: sent(item, leg))

    for mine in (0, 1):

        @pl.when(core == mine)
        def _():
            leave(0, (mine,))
            pl.semaphore_wait(ready, 1)
            leave(0, (1 - mine,))

    own_value = pltpu.make_async_copy(values.at[me], value_out.at[me], own_sem.at[0])
    own_value.start()

    angle_copy.wait()
    for start in range(0, length, 128):
        block = angle[:, start:start + 128]
        c, s = jnp.cos(block), jnp.sin(block)
        cosine[start:start + 128, :] = jnp.concatenate([c, c], axis=0).T
        sine[start:start + 128, :] = jnp.concatenate([-s, s], axis=0).T

    def turn(b, _):
        pltpu.make_async_copy(keys.at[b], raw.at[b], raw_sem.at[b]).wait()

        def tile(i, _):
            rows = pl.ds(pl.multiple_of(i * 128, 128), 128)
            x = raw[b, rows, :].astype(jnp.float32)
            turned[b, rows, :] = (x * cosine[rows, :] + pltpu.roll(x, 64, 1) * sine[rows, :]).astype(jnp.bfloat16)
            return 0

        return lax.fori_loop(0, length // 128, tile, 0)

    lax.fori_loop(0, 16, turn, 0)
    hold(0, 0)
    leave(1, (0, 1))
    own_key = pltpu.make_async_copy(turned.at[me], key_out.at[me], own_sem.at[1])
    own_key.start()
    for first in GROUPS:
        forward(1, first)
    for first in GROUPS:
        at.on_late(first, False, lambda: forward(0, first))

    def keep(way, second):
        return pltpu.make_async_copy(
            values.at[place(*both(way, 0, second)), at.rows(way)], value_relay.at[way, 0, second - 1],
            keep_sem.at[way * 3 + second - 1],
        )

    for way in (0, 1):
        for second in FAR_FIRST:
            at.on_late(0, True, lambda: keep(way, second).start())

    own_key.wait()
    for way in (0, 1):
        page_bounds(key_out, me, way, tops, bottoms)
    for first in FAR_FIRST:
        for way in (0, 1):
            hop(1, way, 0, first, 0).wait_recv()
            page_bounds(key_out, place(*both(way, -first, 0)), way, tops, bottoms)
    for first in GROUPS:
        for second in FAR_FIRST:
            for way in (0, 1):
                hop(1, way, 1, first, second).wait_recv()
                page_bounds(key_out, place(*both(way, -first, -second)), way, tops, bottoms)
    high_out[...] = tops[...].astype(jnp.bfloat16)
    low_out[...] = bottoms[...].astype(jnp.bfloat16)
    own_value.wait()

    def relayed(first):
        for second in FAR_FIRST:
            for way in (0, 1):
                if first:
                    hop(0, way, 0, first, second).wait_recv()
                else:
                    keep(way, second).wait()

    def arrive(first):
        for second in FAR_FIRST:
            for way in (0, 1):
                hop(0, way, 1, first, second).wait_recv()
                hop(0, way, 1, first, second).wait_send()

    for way in (0, 1):
        for first in FAR_FIRST:
            hop(0, way, 0, first, 0).wait_recv()
    pl.when(core == 0)(lambda: sent(0, 0))
    sent(1, 0)
    sent(1, 1)
    for first in GROUPS:
        at.on_late(first, True, lambda: relayed(first))
        at.on_late(first, False, lambda: arrive(first))


def last_groups(relay, _, value_out, send_sem, recv_sem):
    at = layout(value_out.shape[1])

    def hop(way, first, second):
        index = (way * 4 + first) * 4 + second
        return pltpu.make_async_remote_copy(
            src_ref=relay.at[way, first, second - 1],
            dst_ref=value_out.at[at.place(*at.both(way, -first, 0)), at.rows(way)],
            send_sem=send_sem.at[index], recv_sem=recv_sem.at[index],
            device_id=at.device(*at.ring(1 - way, second)), device_id_type=MESH,
        )

    @pl.when(at.core == 0)
    def _():
        barrier = pltpu.get_barrier_semaphore()
        for step in (1, 3, 2):
            for way in (0, 1):
                pl.semaphore_signal(barrier, inc=1, device_id=at.device(*at.ring(way, step)), device_id_type=MESH)
        pl.semaphore_wait(barrier, 6)
        groups = [(way, first, second) for first in LATE for second in FAR_FIRST for way in (0, 1)]
        for which in groups:
            hop(*which).start()
        for which in groups:
            hop(*which).wait()


def piece(at, src, dst, sems, way, first, second):
    here = (at.place(*at.both(way, -first, -second)), at.rows(way))
    return pltpu.make_async_copy(src.at[here], dst.at[here], sems.at[(way * 4 + first) * 4 + second])


def write_early(key_in, value_in, high_in, low_in, key_out, value_out, high_out, low_out, done, sems):
    at = layout(key_in.shape[1])
    done[...] = jnp.zeros_like(done)
    copies = [
        pltpu.make_async_copy(key_in.at[pl.ds(4 * part, 4)], key_out.at[pl.ds(4 * part, 4)], sems.at[32 + part])
        for part in range(4)
    ]
    copies.append(pltpu.make_async_copy(high_in, high_out, sems.at[36]))
    copies.append(pltpu.make_async_copy(low_in, low_out, sems.at[37]))
    for copy in copies:
        copy.start()

    def each(first, seconds, act):
        for second in seconds:
            for way in (0, 1):
                act(piece(at, value_in, value_out, sems, way, first, second))

    for act in (lambda copy: copy.start(), lambda copy: copy.wait()):
        for first in GROUPS:
            each(first, (0,), act)
            at.on_late(first, False, lambda: each(first, FAR_FIRST, act))
    for copy in copies:
        copy.wait()


def write_late(_, value_in, value_out, sems):
    at = layout(value_in.shape[1])

    def each(first, act):
        for second in FAR_FIRST:
            for way in (0, 1):
                act(piece(at, value_in, value_out, sems, way, first, second))

    for act in (lambda copy: copy.start(), lambda copy: copy.wait()):
        for first in GROUPS:
            at.on_late(first, True, lambda: each(first, act))


def on_device(fresh_keys, fresh_values, turn_angle):
    batch, length, _, size = fresh_keys.shape
    half_head = turn_angle.shape[1]
    pages = batch * length // PAGE
    vmem, any_space = pl.BlockSpec(memory_space=pltpu.VMEM), pl.BlockSpec(memory_space=pl.ANY)
    whole, bounds = (batch, length, size), (pages, size)
    relay = (SIDE - 1, length // 2, size)
    early_keys, early_values, value_relay, high, low = pl.pallas_call(
        exchange,
        out_shape=(
            pltpu.VMEM(whole, jnp.bfloat16),
            pltpu.VMEM(whole, jnp.bfloat16),
            pltpu.VMEM((2, SIDE) + relay, jnp.bfloat16),
            pltpu.VMEM(bounds, jnp.bfloat16),
            pltpu.VMEM(bounds, jnp.bfloat16),
        ),
        in_specs=[any_space] * 3,
        out_specs=(vmem,) * 5,
        scratch_shapes=[
            pltpu.VMEM(whole, jnp.bfloat16),
            pltpu.VMEM(whole, jnp.bfloat16),
            pltpu.VMEM((2, SIDE - 1) + relay, jnp.bfloat16),
            pltpu.VMEM(bounds, jnp.float32),
            pltpu.VMEM(bounds, jnp.float32),
            pltpu.VMEM((half_head, length), jnp.float32),
            pltpu.VMEM((length, size), jnp.float32),
            pltpu.VMEM((length, size), jnp.float32),
            pltpu.SemaphoreType.DMA((128,)),
            pltpu.SemaphoreType.DMA((128,)),
            pltpu.SemaphoreType.DMA((16,)),
            pltpu.SemaphoreType.DMA((2,)),
            pltpu.SemaphoreType.DMA,
            pltpu.SemaphoreType.DMA((6,)),
            pltpu.SemaphoreType.REGULAR,
        ],
        compiler_params=pltpu.CompilerParams(
            collective_id=0, has_side_effects=True, vmem_limit_bytes=43 * 2**20
        ),
    )(fresh_keys.reshape(whole), fresh_values.reshape(whole), turn_angle.T)
    cache_keys, some_values, high, low, written = pl.pallas_call(
        write_early,
        out_shape=(
            jax.ShapeDtypeStruct(whole, jnp.bfloat16),
            jax.ShapeDtypeStruct(whole, jnp.bfloat16),
            jax.ShapeDtypeStruct(bounds, jnp.bfloat16),
            jax.ShapeDtypeStruct(bounds, jnp.bfloat16),
            pltpu.VMEM((8, size), jnp.float32),
        ),
        in_specs=[vmem] * 4,
        out_specs=(any_space,) * 4 + (vmem,),
        scratch_shapes=[pltpu.SemaphoreType.DMA((38,))],
        compiler_params=pltpu.CompilerParams(vmem_limit_bytes=2**20),
    )(early_keys, early_values, high, low)
    late_values = pl.pallas_call(
        last_groups,
        out_shape=pltpu.VMEM(whole, jnp.bfloat16),
        in_specs=[vmem] * 2,
        out_specs=vmem,
        scratch_shapes=[pltpu.SemaphoreType.DMA((32,)), pltpu.SemaphoreType.DMA((32,))],
        compiler_params=pltpu.CompilerParams(
            collective_id=1, has_side_effects=True, vmem_limit_bytes=4 * 2**20
        ),
    )(value_relay, written)
    cache_values = pl.pallas_call(
        write_late,
        out_shape=jax.ShapeDtypeStruct(whole, jnp.bfloat16),
        in_specs=[any_space, vmem],
        out_specs=any_space,
        input_output_aliases={0: 0},
        scratch_shapes=[pltpu.SemaphoreType.DMA((32,))],
        compiler_params=pltpu.CompilerParams(vmem_limit_bytes=2**20),
    )(some_values, late_values)
    return (
        cache_keys.reshape(1, -1, 1, size),
        cache_values.reshape(1, -1, 1, size),
        high.reshape(1, -1, 1, size),
        low.reshape(1, -1, 1, size),
    )


def solution(mesh):
    cut = P(None, ("coarse", "fine"), "model", None)
    whole = P(("coarse", "fine"), None, "model", None)
    return jax.shard_map(
        on_device, mesh=mesh, in_specs=(cut, cut, P()), out_specs=(whole,) * 4, check_vma=False
    )
```

time: 146 us -> 145 us (level)
    pallas_call x2, Pallas kernels: 29.1 us -> 22.7 us  [the longest x1 20.6 us: on_device(): pl.pallas_call(last_groups, out_shape=pltpu.VMEM(whole, jnp.bfloat16), in...]
    pallas_call x1, Pallas kernels: 113 us -> 118 us  [on_device(): pl.pallas_call(exchange, out_shape=(pltpu.VMEM(whole, jnp.bfloat16), pltp...]
where the time goes in v5:
time: 145 us
  Pallas kernels  145 us (100%)
    pallas_call x1, Pallas kernels, on_device(): pl.pallas_call(exchange, out_shape=(pltpu.VMEM(whole, jnp.bfloat16), pltp...  118 us
    pallas_call x1, Pallas kernels, on_device(): pl.pallas_call(last_groups, out_shape=pltpu.VMEM(whole, jnp.bfloat16), in...  20.6 us
    pallas_call x1, Pallas kernels, on_device(): pl.pallas_call(write_early, out_shape=(jax.ShapeDtypeStruct(whole, jnp.bf...  3.94 us

profile of v5, /device:TPU:0, one launch (start us, length us, event | category | flops | bytes accessed | tf_op | source)
XLA Modules:
  0.0 145.3 jit_solution(14532507140208763264)
XLA Ops:
  0.6 118.0 %shard_map.66 = (bf16[16,1536,128]{2,1,0:T(8,128)(2,1)S(1)}, bf16[16,1536,128]{2,1,0:T(8,128)(2,1)S(1)}, bf16[2,4,3,768,128]{4,3,2,1,0:T(8,128)(2,1)S(1)}, bf16[...) custom-call(bf16[16,1536,128]{2,1,0:T(8,128)(2,1)} %bitcast.7, bf16[16,1536,128]{2,1,0:T(8,128)(2,1)} %bitcast.8, ...), custom_call_target="tpu_custom_call" | custom-call | tf_op jit(solution)/shard_map/pallas_call | solution.py:312
  118.6 3.9 %shard_map.67 = (bf16[16,1536,128]{2,1,0:T(8,128)(2,1)}, bf16[16,1536,128]{2,1,0:T(8,128)(2,1)}, bf16[768,128]{1,0:T(8,128)(2,1)}, bf16[768,128]{1,0:T(8,128)(2,1)}, f32[8,128]{1,0:T(8,128)S(1)}) custom-call(bf16[16,1536,128]{2,1,0:T(8,128)(2,1)S(1)} %get-tuple-element.14.key_in, bf16[16,1536,128]{2,1,0:T(8,128)(2,1)S(1)} %get-tuple-element.15.value_in, ...), custom_call_target="tpu_custom_call" | custom-call | tf_op jit(solution)/shard_map/pallas_call | solution.py:344
  122.5 20.6 %shard_map.68.value_in = bf16[16,1536,128]{2,1,0:T(8,128)(2,1)S(1)} custom-call(bf16[2,4,3,768,128]{4,3,2,1,0:T(8,128)(2,1)S(1)} %get-tuple-element.20.relay, f32[8,128]{1,0:T(8,128)S(1)} %get-tuple-element.21._), custom_call_target="tpu_custom_call" | custom-call | tf_op jit(solution)/shard_map/pallas_call | solution.py:358
  143.2 2.1 %shard_map.69 = bf16[16,1536,128]{2,1,0:T(8,128)(2,1)} custom-call(bf16[16,1536,128]{2,1,0:T(8,128)(2,1)} %get-tuple-element.19._, bf16[16,1536,128]{2,1,0:T(8,128)(2,1)S(1)} %shard_map.68.value_in), custom_call_target="tpu_custom_call", output_to_operand_aliasing={{}: (0, {})} | custom-call | tf_op jit(solution)/shard_map/pallas_call | solution.py:368

commit v6 on v5

--- a/solution.py
+++ b/solution.py
@@ -140,9 +140,6 @@
                 for second in FAR_FIRST if leg else range(4):
                     hop(item, way, leg, first, second).wait_send()
 
-    def hold(item, leg):
-        pl.when(core == 1)(lambda: sent(item, leg))
-
     for mine in (0, 1):
 
         @pl.when(core == mine)
@@ -173,8 +170,20 @@
         return lax.fori_loop(0, length // 128, tile, 0)
 
     lax.fori_loop(0, 16, turn, 0)
-    hold(0, 0)
-    leave(1, (0, 1))
+    @pl.when(core == 0)
+    def _():
+        leave(1, (0, 1))
+
+    @pl.when(core == 1)
+    def _():
+        sent(0, 0)
+        for second in (1, 2, 3, 0):
+            batch = [hop(1, way, 0, first, second) for first in FAR_FIRST for way in (0, 1)]
+            for copy in batch:
+                copy.start()
+            for copy in batch:
+                copy.wait_send()
+
     own_key = pltpu.make_async_copy(turned.at[me], key_out.at[me], own_sem.at[1])
     own_key.start()
     for first in GROUPS:
@@ -226,7 +235,7 @@
         for first in FAR_FIRST:
             hop(0, way, 0, first, 0).wait_recv()
     pl.when(core == 0)(lambda: sent(0, 0))
-    sent(1, 0)
+    pl.when(core == 0)(lambda: sent(1, 0))
     sent(1, 1)
     for first in GROUPS:
         at.on_late(first, True, lambda: relayed(first))

time: 145 us -> 145 us (level)
    pallas_call x1, Pallas kernels: 118 us -> 115 us  [on_device(): pl.pallas_call(exchange, out_shape=(pltpu.VMEM(whole, jnp.bfloat16), pltp...]
    pallas_call x1, Pallas kernels: 20.6 us -> 23.2 us  [on_device(): pl.pallas_call(last_groups, out_shape=pltpu.VMEM(whole, jnp.bfloat16), in...]
where the time goes in v6:
time: 145 us
  Pallas kernels  144 us (99%)
    pallas_call x1, Pallas kernels, on_device(): pl.pallas_call(exchange, out_shape=(pltpu.VMEM(whole, jnp.bfloat16), pltp...  115 us
    pallas_call x1, Pallas kernels, on_device(): pl.pallas_call(last_groups, out_shape=pltpu.VMEM(whole, jnp.bfloat16), in...  23.2 us
    pallas_call x1, Pallas kernels, on_device(): pl.pallas_call(write_early, out_shape=(jax.ShapeDtypeStruct(whole, jnp.bf...  3.94 us

profile of v6, /device:TPU:0, one launch (start us, length us, event | category | flops | bytes accessed | tf_op | source)
XLA Modules:
  0.0 145.1 jit_solution(6677650158518693920)
XLA Ops:
  0.6 115.3 %shard_map.66 = (bf16[16,1536,128]{2,1,0:T(8,128)(2,1)S(1)}, bf16[16,1536,128]{2,1,0:T(8,128)(2,1)S(1)}, bf16[2,4,3,768,128]{4,3,2,1,0:T(8,128)(2,1)S(1)}, bf16[...) custom-call(bf16[16,1536,128]{2,1,0:T(8,128)(2,1)} %bitcast.7, bf16[16,1536,128]{2,1,0:T(8,128)(2,1)} %bitcast.8, ...), custom_call_target="tpu_custom_call" | custom-call | tf_op jit(solution)/shard_map/pallas_call | solution.py:321
  115.9 3.9 %shard_map.67 = (bf16[16,1536,128]{2,1,0:T(8,128)(2,1)}, bf16[16,1536,128]{2,1,0:T(8,128)(2,1)}, bf16[768,128]{1,0:T(8,128)(2,1)}, bf16[768,128]{1,0:T(8,128)(2,1)}, f32[8,128]{1,0:T(8,128)S(1)}) custom-call(bf16[16,1536,128]{2,1,0:T(8,128)(2,1)S(1)} %get-tuple-element.14.key_in, bf16[16,1536,128]{2,1,0:T(8,128)(2,1)S(1)} %get-tuple-element.15.value_in, ...), custom_call_target="tpu_custom_call" | custom-call | tf_op jit(solution)/shard_map/pallas_call | solution.py:353
  119.8 23.2 %shard_map.68.value_in = bf16[16,1536,128]{2,1,0:T(8,128)(2,1)S(1)} custom-call(bf16[2,4,3,768,128]{4,3,2,1,0:T(8,128)(2,1)S(1)} %get-tuple-element.20.relay, f32[8,128]{1,0:T(8,128)S(1)} %get-tuple-element.21._), custom_call_target="tpu_custom_call" | custom-call | tf_op jit(solution)/shard_map/pallas_call | solution.py:367
  143.0 2.1 %shard_map.69 = bf16[16,1536,128]{2,1,0:T(8,128)(2,1)} custom-call(bf16[16,1536,128]{2,1,0:T(8,128)(2,1)} %get-tuple-element.19._, bf16[16,1536,128]{2,1,0:T(8,128)(2,1)S(1)} %shard_map.68.value_in), custom_call_target="tpu_custom_call", output_to_operand_aliasing={{}: (0, {})} | custom-call | tf_op jit(solution)/shard_map/pallas_call | solution.py:377

commit v7 on v5

--- a/solution.py
+++ b/solution.py
@@ -177,6 +177,7 @@
     leave(1, (0, 1))
     own_key = pltpu.make_async_copy(turned.at[me], key_out.at[me], own_sem.at[1])
     own_key.start()
+    hold(1, 0)
     for first in GROUPS:
         forward(1, first)
     for first in GROUPS:
@@ -226,7 +227,7 @@
         for first in FAR_FIRST:
             hop(0, way, 0, first, 0).wait_recv()
     pl.when(core == 0)(lambda: sent(0, 0))
-    sent(1, 0)
+    pl.when(core == 0)(lambda: sent(1, 0))
     sent(1, 1)
     for first in GROUPS:
         at.on_late(first, True, lambda: relayed(first))

time: 145 us -> 145 us (level)
  no operation moved by 1% of the time
where the time goes in v7:
time: 145 us
  Pallas kernels  145 us (100%)
    pallas_call x1, Pallas kernels, on_device(): pl.pallas_call(exchange, out_shape=(pltpu.VMEM(whole, jnp.bfloat16), pltp...  117 us
    pallas_call x1, Pallas kernels, on_device(): pl.pallas_call(last_groups, out_shape=pltpu.VMEM(whole, jnp.bfloat16), in...  21.3 us
    pallas_call x1, Pallas kernels, on_device(): pl.pallas_call(write_early, out_shape=(jax.ShapeDtypeStruct(whole, jnp.bf...  3.94 us

profile of v7, /device:TPU:0, one launch (start us, length us, event | category | flops | bytes accessed | tf_op | source)
XLA Modules:
  0.0 145.2 jit_solution(8674410323308121265)
XLA Ops:
  0.6 117.2 %shard_map.66 = (bf16[16,1536,128]{2,1,0:T(8,128)(2,1)S(1)}, bf16[16,1536,128]{2,1,0:T(8,128)(2,1)S(1)}, bf16[2,4,3,768,128]{4,3,2,1,0:T(8,128)(2,1)S(1)}, bf16[...) custom-call(bf16[16,1536,128]{2,1,0:T(8,128)(2,1)} %bitcast.7, bf16[16,1536,128]{2,1,0:T(8,128)(2,1)} %bitcast.8, ...), custom_call_target="tpu_custom_call" | custom-call | tf_op jit(solution)/shard_map/pallas_call | solution.py:313
  117.8 3.9 %shard_map.67 = (bf16[16,1536,128]{2,1,0:T(8,128)(2,1)}, bf16[16,1536,128]{2,1,0:T(8,128)(2,1)}, bf16[768,128]{1,0:T(8,128)(2,1)}, bf16[768,128]{1,0:T(8,128)(2,1)}, f32[8,128]{1,0:T(8,128)S(1)}) custom-call(bf16[16,1536,128]{2,1,0:T(8,128)(2,1)S(1)} %get-tuple-element.14.key_in, bf16[16,1536,128]{2,1,0:T(8,128)(2,1)S(1)} %get-tuple-element.15.value_in, ...), custom_call_target="tpu_custom_call" | custom-call | tf_op jit(solution)/shard_map/pallas_call | solution.py:345
  121.8 21.3 %shard_map.68.value_in = bf16[16,1536,128]{2,1,0:T(8,128)(2,1)S(1)} custom-call(bf16[2,4,3,768,128]{4,3,2,1,0:T(8,128)(2,1)S(1)} %get-tuple-element.20.relay, f32[8,128]{1,0:T(8,128)S(1)} %get-tuple-element.21._), custom_call_target="tpu_custom_call" | custom-call | tf_op jit(solution)/shard_map/pallas_call | solution.py:359
  143.1 2.1 %shard_map.69 = bf16[16,1536,128]{2,1,0:T(8,128)(2,1)} custom-call(bf16[16,1536,128]{2,1,0:T(8,128)(2,1)} %get-tuple-element.19._, bf16[16,1536,128]{2,1,0:T(8,128)(2,1)S(1)} %shard_map.68.value_in), custom_call_target="tpu_custom_call", output_to_operand_aliasing={{}: (0, {})} | custom-call | tf_op jit(solution)/shard_map/pallas_call | solution.py:369
